TPU v7x, 64 devices: a 2x2x8 block of a 4x4x8 slice. The times are simulated.
64 devices in a mesh: sys: 4 (over x, y), seg: 16 (over z, core).
Axes of the slice: x: 2, y: 2, z: 8, core: 2. Of those that a mesh axis runs over, the one named last changes fastest.
The devices are a block of a 4x4x8 slice.
Arguments:
- positions: bfloat16 [196608, 320], P(('sys', 'seg')), parts along dimension 0
- charges: float32 [196608], P(('sys', 'seg')), parts along dimension 0
- pair_band: int32 [64, 15], P(('sys', 'seg')), parts along dimension 0
Outputs:
- output 1: float32 [196608, 320], P(('sys', 'seg')), parts along dimension 0
- output 2: float32 [4], P('sys'), parts along dimension 0
There are 4 independent parts. A program takes and returns all parts, laid end to end along the dimension named above; each array names one.
All inputs are finite; a program needn't handle non-finite values.
Results may differ from a plain program's by a relative error of at most 0.001.
Values are sent between devices in bfloat16 or wider.
A program may use at most 768 MiB of HBM per device.

v0:
```python
import functools
import math

import jax
import jax.numpy as jnp
from jax import lax
from jax.experimental import pallas as pl
from jax.experimental.pallas import tpu as pltpu
from jax.sharding import PartitionSpec as P

CHUNKS = 6
TILE = 256
EXTRA = 8
DEPTH = 384
MESH = pl.DeviceIdType.MESH

SQUARE, CHARGE, HOST_CHARGE = 0, 3, 11


def pieces(values):
    high = values.astype(jnp.bfloat16).astype(jnp.float32)
    rest = values - high
    mid = rest.astype(jnp.bfloat16).astype(jnp.float32)
    return [high, mid, rest - mid]


def pack_kernel(chunks, x_ref, q_ref, *out_refs):
    feat = x_ref.shape[0]
    width = out_refs[0].shape[-1]
    for chunk in chunks:
        cols = slice(chunk * width, (chunk + 1) * width)
        x = x_ref[:, cols]
        xf = x.astype(jnp.float32)
        square = jnp.minimum(jnp.sum(xf * xf, axis=0, keepdims=True), 3.0e38)
        extra = jnp.concatenate(pieces(square) + pieces(q_ref[:, cols]) + [jnp.zeros((EXTRA - 6, width), jnp.float32)], axis=0)
        extra = extra.astype(jnp.bfloat16)
        targets = out_refs if len(chunks) == 1 else [out_refs[-1].at[chunk]] + ([out_refs[chunk - 1]] if chunk else [])
        for ref in targets:
            ref[:feat, :] = x
            ref[feat:, :] = extra


def lower_rows(feat, width):
    n_low = DEPTH - feat - EXTRA
    row = lax.broadcasted_iota(jnp.int32, (n_low, width), 0)
    return jnp.where(row < 3, 1.0, 0.0).astype(jnp.bfloat16)


def pair_task(vis_ref, host, gap, keep, host_ref, charge_ref, acc_ref, sum_ref):
    feat, half = acc_ref.shape[1:]
    width = vis_ref.shape[1]
    scale = -math.log2(math.e) * 0.5 / feat
    extra = vis_ref[feat:feat + EXTRA, :].astype(jnp.float32)
    charge_j = extra[CHARGE:CHARGE + 1] + extra[CHARGE + 1:CHARGE + 2] + extra[CHARGE + 2:CHARGE + 3]
    if keep is not None:
        charge_j = jnp.where(keep, charge_j, 0.0)

    def span(tile):
        return slice(tile * TILE, (tile + 1) * TILE)

    def distance(tile):
        return jnp.dot(host_ref[host, span(tile), :], vis_ref[...], preferred_element_type=jnp.float32)

    def pull(weights, tile):
        acc_ref[host, :, span(tile)] += lax.dot_general(
            vis_ref[:feat, :], weights, (((1,), (1,)), ((), ())), preferred_element_type=jnp.float32)

    n_tiles = half // TILE
    ahead = distance(0)
    behind = None
    for tile in range(n_tiles):
        charge_i = jnp.concatenate([charge_ref[host, span(tile), :]] * (width // 128), axis=1)
        weights = jnp.exp2(jnp.maximum(ahead, 0.0) * scale) * charge_i * charge_j
        if gap is not None:
            row = lax.broadcasted_iota(jnp.int32, weights.shape, 0)
            col = lax.broadcasted_iota(jnp.int32, weights.shape, 1)
            weights = jnp.where(col - row == gap + tile * TILE, 0.0, weights)
        part = weights[:, :128]
        for group in range(1, width // 128):
            part = part + weights[:, group * 128:(group + 1) * 128]
        sum_ref[host, span(tile), :] += part
        if tile + 1 < n_tiles:
            ahead = distance(tile + 1)
        if behind is not None:
            pull(behind, tile - 1)
        behind = weights.astype(jnp.bfloat16)
    pull(behind, n_tiles - 1)


def sweep(acc_ref, sum_ref, step):
    for number, ref, rows in ((0, acc_ref, 8), (1, sum_ref, 96)):
        def one(k, carry):
            step(number, (slice(None), pl.ds(pl.multiple_of(k * rows, 8), rows), slice(None)))
            return carry

        lax.fori_loop(0, ref.shape[1] // rows, one, 0)


def clear_sums(acc_ref, sum_ref):
    refs = (acc_ref, sum_ref)

    def step(number, rows):
        refs[number][rows] = jnp.zeros_like(refs[number][rows])

    sweep(acc_ref, sum_ref, step)


def host_charges(host_ref, charge_ref, feat):
    base = DEPTH - 128
    row = lax.broadcasted_iota(jnp.int32, (128, 128), 0) + base - feat - HOST_CHARGE
    pick = jnp.where((row >= 0) & (row < 3), 1.0, 0.0).astype(jnp.bfloat16)
    for host in range(2):
        charge_ref[host] = jnp.dot(host_ref[host, :, base:], pick, preferred_element_type=jnp.float32)


def near_kernel(seg_len, reach, band_ref, own_ref, partner_ref, list_ref, host_ref, acc_ref, sum_ref, vis, charges, sems):
    feat = own_ref.shape[1] - EXTRA
    width = own_ref.shape[2]
    half = CHUNKS * width // 2
    per_half = CHUNKS // 2
    me = lax.axis_index('seg')
    core = lax.rem(me, 2)
    copies = []
    for side, ref in enumerate((own_ref, partner_ref)):
        for chunk in range(CHUNKS):
            slot = side * CHUNKS + chunk
            copies.append(pltpu.make_async_copy(ref.at[chunk], vis.at[slot, pl.ds(0, feat + EXTRA), :], sems.at[slot]))
            copies[-1].start()
    low = lower_rows(feat, width)
    for slot in range(2 * CHUNKS):
        vis[slot, feat + EXTRA:, :] = low
    clear_sums(acc_ref, sum_ref)

    n_list = 2 * seg_len
    list_ref[0] = 0

    def clear(i, carry):
        list_ref[i] = 0
        return carry

    lax.fori_loop(0, list_ref.shape[0], clear, 0)
    for host in range(2):
        block = me if host == 0 else me + 1 - 2 * core

        def add(other, count):
            step = lax.rem(other - block + seg_len + seg_len // 2, seg_len) - seg_len // 2
            inside = (step >= -reach) & (step <= reach) & (other // 2 != me // 2)
            live = inside & (band_ref[host, jnp.clip(step + reach, 0, 2 * reach)] != 0)

            @pl.when(live)
            def _():
                list_ref[1 + count] = other
                list_ref[1 + n_list + 2 + count] = host

            return count + live.astype(jnp.int32)

        list_ref[0] = lax.fori_loop(0, seg_len, add, list_ref[0])

    for copy in copies:
        copy.wait()
    for host in range(2):
        for part in range(per_half):
            slot = host * CHUNKS + core * per_half + part
            block = vis[slot]
            extra = block[feat:feat + EXTRA].astype(jnp.float32)
            n_low = DEPTH - feat - EXTRA
            upper = jnp.concatenate([jnp.ones((3, width), jnp.float32), jnp.zeros((EXTRA - 3, width), jnp.float32)], axis=0)
            lower = jnp.concatenate([
                extra[SQUARE:SQUARE + 3], extra[CHARGE:CHARGE + 3], jnp.zeros((n_low - 6, width), jnp.float32)], axis=0)
            below = jnp.concatenate([upper, lower], axis=0).astype(jnp.bfloat16)
            full = jnp.concatenate([-2 * block[:feat], below], axis=0)
            host_ref[host, part * width:(part + 1) * width, :] = full.T
    host_charges(host_ref, charges, feat)

    def run(slot, host, gap):
        pair_task(vis.at[slot], host, gap, None, host_ref, charges, acc_ref, sum_ref)

    def masked(step, carry):
        host = step // per_half
        part = lax.rem(step, per_half)
        run(host * CHUNKS + core * per_half + part, host, -part * width)
        return carry

    def unmasked(step, carry):
        far_step = step - CHUNKS
        host = jnp.where(step < CHUNKS, step // per_half, far_step // CHUNKS)
        base = jnp.where(step < CHUNKS, host * CHUNKS + (1 - core) * per_half + lax.rem(step, per_half), (1 - host) * CHUNKS + lax.rem(step, CHUNKS))
        run(base, host, None)
        return carry

    lax.fori_loop(0, CHUNKS, masked, 0)
    linked = band_ref[0, reach + 1 - 2 * core] != 0
    lax.fori_loop(0, jnp.where(linked, 3 * CHUNKS, CHUNKS), unmasked, 0)


def far_kernel(last, list_ref, vis_ref, host_ref, acc_old, sum_old, *refs):
    if last:
        own_ref, partner_ref, acc_ref, energy_ref, vis, charges, acc_prev, sum_prev, sems, old_sems, sum_ref, x_buf, x_sems = refs
    else:
        acc_ref, sum_ref, vis, charges, acc_prev, sum_prev, sems, old_sems = refs
    feat = acc_ref.shape[1]
    width = vis.shape[3]
    n_list = (list_ref.shape[0] - 1) // 2
    count = list_ref[0]
    old = [pltpu.make_async_copy(acc_old, acc_prev, old_sems.at[0]), pltpu.make_async_copy(sum_old, sum_prev, old_sems.at[1])]

    def fetch(pair, slot):
        return [pltpu.make_async_copy(
            vis_ref.at[list_ref[1 + 2 * pair + u]], vis.at[slot, u, pl.ds(0, feat + EXTRA), :], sems.at[slot, u]) for u in range(2)]

    if last:
        per_half = acc_ref.shape[2] // width
        core = lax.rem(lax.axis_index('seg'), 2)
        for host, ref in enumerate((own_ref, partner_ref)):
            for part in range(per_half):
                old.append(pltpu.make_async_copy(
                    ref.at[core * per_half + part, pl.ds(0, feat), :], x_buf.at[host, :, pl.ds(part * width, width)], x_sems.at[host, part]))
    for copy in fetch(0, 0) + old:
        copy.start()
    low = lower_rows(feat, width)
    for slot in range(2):
        for u in range(2):
            vis[slot, u, feat + EXTRA:, :] = low
    clear_sums(acc_ref, sum_ref)
    host_charges(host_ref, charges, feat)

    def run(slot, u, task):
        pair_task(vis.at[slot, u], list_ref[1 + n_list + task], None, (task < count) if u else None, host_ref, charges, acc_ref, sum_ref)

    def two_tasks(pair, carry):
        slot = lax.rem(pair, 2)
        for copy in fetch(pair, slot):
            copy.wait()
        for copy in fetch(pair + 1, 1 - slot):
            copy.start()
        for u in range(2):
            run(slot, u, 2 * pair + u)
        return carry

    pairs = (count + 1) // 2
    lax.fori_loop(0, pairs, two_tasks, 0)
    for copy in fetch(pairs, lax.rem(pairs, 2)):
        copy.wait()

    for copy in old:
        copy.wait()
    if not last:
        def step(number, rows):
            (acc_ref, sum_ref)[number][rows] += (acc_prev, sum_prev)[number][rows]

        sweep(acc_ref, sum_ref, step)
        return
    half = acc_ref.shape[2]
    energy = jnp.zeros((8, 128), jnp.float32)
    for host in range(2):
        sums = sum_ref[host] + sum_prev[host]
        energy = energy + jnp.sum(sums.reshape(half // 8, 8, 128), axis=0)
        total = jnp.zeros((8, half), jnp.float32)
        for piece in pieces(sums):
            total = total + lax.dot_general(
                jnp.ones((8, 128), jnp.bfloat16), piece.astype(jnp.bfloat16), (((1,), (1,)), ((), ())), preferred_element_type=jnp.float32)
        pulled = acc_ref[host] + acc_prev[host]
        acc_ref[host] = (total[0:1] * x_buf[host].astype(jnp.float32) - pulled) * (1.0 / feat)
    energy_ref[...] = energy


def join_kernel(mine_ref, other_ref, out_ref, bounce, sems):
    half = other_ref.shape[1]
    core = lax.rem(lax.axis_index('seg'), 2)
    sources = [mine_ref.at[0], other_ref]
    loads = [pltpu.make_async_copy(sources[k], bounce.at[k], sems.at[0, k]) for k in range(2)]
    for load in loads:
        load.start()
    stores = []
    for k in range(2):
        place = pl.multiple_of((core if k == 0 else 1 - core) * half, 128)
        loads[k].wait()
        stores.append(pltpu.make_async_copy(bounce.at[k], out_ref.at[:, pl.ds(place, half)], sems.at[1, k]))
        stores[-1].start()
    for store in stores:
        store.wait()


def total_kernel(n, x_ref, out_ref, slots, send_sems, recv_sems):
    me = lax.axis_index('seg')
    barrier = pltpu.get_barrier_semaphore()
    for k in range(1, n):
        pl.semaphore_signal(barrier, inc=1, device_id={'seg': lax.rem(me + k, n)}, device_id_type=MESH)
    pl.semaphore_wait(barrier, n - 1)
    sends = []
    for k in range(1, n):
        sends.append(pltpu.make_async_remote_copy(
            src_ref=x_ref, dst_ref=slots.at[me], send_sem=send_sems.at[k], recv_sem=recv_sems.at[me],
            device_id={'seg': lax.rem(me + k, n)}, device_id_type=MESH))
        sends[-1].start()
    slots[me] = x_ref[...]
    for k in range(1, n):
        owner = lax.rem(me + k, n)
        pltpu.make_async_remote_copy(
            src_ref=x_ref, dst_ref=slots.at[owner], send_sem=send_sems.at[k], recv_sem=recv_sems.at[owner],
            device_id={'seg': owner}, device_id_type=MESH).wait_recv()
    for send in sends:
        send.wait_send()
    total = slots[0]
    for k in range(1, n):
        total = total + slots[k]
    out_ref[...] = total


def solution(mesh):
    seg_len = mesh.shape['seg']
    swap = [(dev, dev ^ 1) for dev in range(seg_len)]
    any_space = pl.BlockSpec(memory_space=pl.ANY)
    vmem = pl.BlockSpec(memory_space=pltpu.VMEM)
    smem = pl.BlockSpec(memory_space=pltpu.SMEM)

    def device_fn(positions, charges, pair_band):
        n_rows, feat = positions.shape
        reach = (pair_band.shape[1] - 1) // 2
        half = n_rows // 2
        width = n_rows // CHUNKS
        shape = jax.ShapeDtypeStruct
        big = pltpu.CompilerParams(vmem_limit_bytes=60 * 2 ** 20)
        packed = (feat + EXTRA, width)

        x_t = positions.T
        charge_row = charges[None, :]
        first_part = pl.pallas_call(
            functools.partial(pack_kernel, (0,)),
            grid=(1,),
            out_shape=shape(packed, jnp.bfloat16),
            in_specs=[pl.BlockSpec((feat, width), lambda i: (0, 0)), pl.BlockSpec((1, width), lambda i: (0, 0))],
            out_specs=pl.BlockSpec(packed, lambda i: (0, 0)),
            name='pack_first',
        )(x_t, charge_row)
        *parts, own = pl.pallas_call(
            functools.partial(pack_kernel, tuple(range(CHUNKS))),
            out_shape=[shape(packed, jnp.bfloat16)] * (CHUNKS - 1) + [shape((CHUNKS,) + packed, jnp.bfloat16)],
            in_specs=[vmem, vmem],
            out_specs=[vmem] * CHUNKS,
            compiler_params=big,
            name='pack',
        )(x_t, charge_row)
        parts = [first_part] + parts
        gathered = [lax.all_gather(part, 'seg') for part in parts]
        partner = lax.ppermute(own, 'seg', swap)
        bands = jnp.concatenate([pair_band, lax.ppermute(pair_band, 'seg', swap)])

        acc_shape = shape((2, feat, half), jnp.float32)
        sum_shape = shape((2, half, 128), jnp.float32)
        host_shape = shape((2, half, DEPTH), jnp.bfloat16)
        n_list = 2 * seg_len + 2
        pair_flops = 4 * half * width * DEPTH
        tasks, host, acc, sums = pl.pallas_call(
            functools.partial(near_kernel, seg_len, reach),
            out_shape=[shape((1 + 2 * n_list,), jnp.int32), host_shape, acc_shape, sum_shape],
            in_specs=[smem, any_space, any_space],
            out_specs=[smem, vmem, vmem, vmem],
            scratch_shapes=[
                pltpu.VMEM((2 * CHUNKS, DEPTH, width), jnp.bfloat16),
                pltpu.VMEM((2, half, 128), jnp.float32),
                pltpu.SemaphoreType.DMA((2 * CHUNKS,)),
            ],
            compiler_params=big,
            cost_estimate=pl.CostEstimate(flops=16 * pair_flops, bytes_accessed=2 ** 24, transcendentals=16 * half * width),
            name='near_pairs',
        )(bands, own, partner)
        for chunk, block in enumerate(gathered):
            last = chunk == CHUNKS - 1
            scratch = [
                pltpu.VMEM((2, 2, DEPTH, width), jnp.bfloat16),
                pltpu.VMEM((2, half, 128), jnp.float32),
                pltpu.VMEM(acc_shape.shape, jnp.float32),
                pltpu.VMEM(sum_shape.shape, jnp.float32),
                pltpu.SemaphoreType.DMA((2, 2)),
                pltpu.SemaphoreType.DMA((2,)),
            ]
            if last:
                scratch += [
                    pltpu.VMEM(sum_shape.shape, jnp.float32),
                    pltpu.VMEM(acc_shape.shape, jnp.bfloat16),
                    pltpu.SemaphoreType.DMA((2, CHUNKS // 2)),
                ]
            acc, sums = pl.pallas_call(
                functools.partial(far_kernel, last),
                out_shape=[acc_shape, shape((8, 128), jnp.float32) if last else sum_shape],
                in_specs=[smem, any_space, vmem, any_space, any_space] + [any_space] * (2 if last else 0),
                out_specs=[vmem, vmem],
                scratch_shapes=scratch,
                compiler_params=big,
                cost_estimate=pl.CostEstimate(flops=20 * pair_flops, bytes_accessed=2 ** 25, transcendentals=20 * half * width),
                name='last_pairs' if last else 'far_pairs',
            )(tasks, block, host, acc, sums, *((own, partner) if last else ()))

        other = lax.ppermute(acc[1], 'seg', swap)
        energy_all = pl.pallas_call(
            functools.partial(total_kernel, seg_len),
            out_shape=shape((8, 128), jnp.float32),
            in_specs=[vmem],
            out_specs=vmem,
            scratch_shapes=[
                pltpu.VMEM((seg_len, 8, 128), jnp.float32),
                pltpu.SemaphoreType.DMA((seg_len,)),
                pltpu.SemaphoreType.DMA((seg_len,)),
            ],
            compiler_params=pltpu.CompilerParams(collective_id=0, has_side_effects=True),
            name='energy_total',
        )(sums)
        energy = 0.5 * jnp.sum(energy_all)

        forces = pl.pallas_call(
            join_kernel,
            out_shape=shape((feat, n_rows), jnp.float32),
            in_specs=[any_space, any_space],
            out_specs=any_space,
            scratch_shapes=[pltpu.VMEM((2, feat, half), jnp.float32), pltpu.SemaphoreType.DMA((2, 2))],
            name='join_halves',
        )(acc, other)
        return forces.T, energy.reshape(1)

    row_spec = P(('sys', 'seg'), None)
    vec_spec = P(('sys', 'seg'))
    return jax.shard_map(device_fn, mesh=mesh, in_specs=(row_spec, vec_spec, row_spec), out_specs=(row_spec, P('sys')), check_vma=False)
```

profile of v0, /device:TPU:22, one launch (start us, length us, event | category | flops | bytes accessed | tf_op | source)
XLA Modules:
  0.0 321.2 jit_solution(16427183242422354096)
XLA Ops:
  7.3 1.7 pack_first.1
  9.1 3.6 %pack.1 = (bf16[328,512]{1,0:T(8,128)(2,1)}, bf16[328,512]{1,0:T(8,128)(2,1)}, bf16[328,512]{1,0:T(8,128)(2,1)}, bf16[328,512]{1,0:T(8,128)(2,1)}, bf16[328,512]...) custom-call(bf16[320,3072]{1,0:T(8,128)(2,1)} %bitcast.13, f32[1,3072]{1,0:T(1,128)} %bitcast.16), custom_call_target="tpu_custom_call" | custom-call | tf_op jit(solution)/shard_map/pack/pallas_call | solution.py:336
  12.9 0.7 all-gather.19.cloned.1.call-update
  13.7 0.6 all-gather.17.cloned.1.call-update
  14.3 0.6 all-gather.15.cloned.1.call-update
  15.7 3.5 %collective-permute-done = s32[1,15]{1,0:T(1,128)S(1)} collective-permute-done((s32[1,15]{1,0:T(1,128)S(1)}, s32[1,15]{1,0:T(1,128)S(1)}, u32[]{:S(2)}, u32[]{:S(2)}) %collective-permute-start) | collective-permute-done | bytes 92 | tf_op jit(solution)/shard_map/ppermute | solution.py:347
  19.1 0.5 pad_add_fusion.band_ref
  19.7 1.3 copy-done.2
  21.0 46.4 %near_pairs.1 = (s32[69]{0:T(128)}, bf16[2,1536,384]{2,1,0:T(8,128)(2,1)}, f32[2,320,1536]{2,1,0:T(8,128)}, f32[2,1536,128]{2,1,0:T(8,128)}) custom-call(s32[2,15]{1,0:T(2,128)} %pad_add_fusion.band_ref, bf16[6,328,512]{2,1,0:T(8,128)(2,1)} %get-tuple-element.24.own_ref.refs_0_, bf16[6,328,512]{2,1,0:T(8,128)(2,1)} %copy-done.2), custom_call_target="tpu_custom_call" | custom-call | flops 19327352832 | bytes 16777216 | tf_op jit(solution)/shard_map/near_pairs/pallas_call | solution.py:354
  67.4 26.5 %far_pairs.5 = (f32[2,320,1536]{2,1,0:T(8,128)}, f32[2,1536,128]{2,1,0:T(8,128)}) custom-call(s32[69]{0:T(128)} %get-tuple-element.25.list_ref, bf16[16,328,512]{2,1,0:T(8,128)(2,1)} %bitcast.17, bf16[2,1536,384]{2,1,0:T(8,128)(2,1)} %get-tuple-element.27.host_ref, f32[2,320,1536]{2,1,0:T(8,128)} %get-tuple-element.32.acc_old, ...), custom_call_target="tpu_custom_call" | custom-call | flops 24159191040 | bytes 33554432 | tf_op jit(solution)/shard_map/far_pairs/pallas_call | solution.py:384
  94.3 26.6 %far_pairs.6 = (f32[2,320,1536]{2,1,0:T(8,128)}, f32[2,1536,128]{2,1,0:T(8,128)}) custom-call(s32[69]{0:T(128)} %get-tuple-element.25.list_ref, bf16[16,328,512]{2,1,0:T(8,128)(2,1)} %bitcast.21, bf16[2,1536,384]{2,1,0:T(8,128)(2,1)} %get-tuple-element.27.host_ref, f32[2,320,1536]{2,1,0:T(8,128)} %get-tuple-element.34.acc_old, ...), custom_call_target="tpu_custom_call" | custom-call | flops 24159191040 | bytes 33554432 | tf_op jit(solution)/shard_map/far_pairs/pallas_call | solution.py:384
  120.9 14.0 %all-gather.19.cloned.1.call-done = bf16[5248,512]{1,0:T(8,128)(2,1)} async-done(((bf16[328,512]{1,0:T(8,128)(2,1)}), bf16[5248,512]{1,0:T(8,128)(2,1)}) %all-gather.19.cloned.1.call-update) | async-done | bytes 5373968 | tf_op jit(solution)/shard_map/all_gather | solution.py:345
  134.9 26.5 %far_pairs.7 = (f32[2,320,1536]{2,1,0:T(8,128)}, f32[2,1536,128]{2,1,0:T(8,128)}) custom-call(s32[69]{0:T(128)} %get-tuple-element.25.list_ref, bf16[16,328,512]{2,1,0:T(8,128)(2,1)} %bitcast.20, bf16[2,1536,384]{2,1,0:T(8,128)(2,1)} %get-tuple-element.27.host_ref, f32[2,320,1536]{2,1,0:T(8,128)} %get-tuple-element.36.acc_old, ...), custom_call_target="tpu_custom_call" | custom-call | flops 24159191040 | bytes 33554432 | tf_op jit(solution)/shard_map/far_pairs/pallas_call | solution.py:384
  161.4 13.9 %all-gather.17.cloned.1.call-done = bf16[5248,512]{1,0:T(8,128)(2,1)} async-done(((bf16[328,512]{1,0:T(8,128)(2,1)}), bf16[5248,512]{1,0:T(8,128)(2,1)}) %all-gather.17.cloned.1.call-update) | async-done | bytes 5373968 | tf_op jit(solution)/shard_map/all_gather | solution.py:345
  175.3 26.5 %far_pairs.8 = (f32[2,320,1536]{2,1,0:T(8,128)}, f32[2,1536,128]{2,1,0:T(8,128)}) custom-call(s32[69]{0:T(128)} %get-tuple-element.25.list_ref, bf16[16,328,512]{2,1,0:T(8,128)(2,1)} %bitcast.19, bf16[2,1536,384]{2,1,0:T(8,128)(2,1)} %get-tuple-element.27.host_ref, f32[2,320,1536]{2,1,0:T(8,128)} %get-tuple-element.38.acc_old, ...), custom_call_target="tpu_custom_call" | custom-call | flops 24159191040 | bytes 33554432 | tf_op jit(solution)/shard_map/far_pairs/pallas_call | solution.py:384
  201.8 13.9 %all-gather.15.cloned.1.call-done = bf16[5248,512]{1,0:T(8,128)(2,1)} async-done(((bf16[328,512]{1,0:T(8,128)(2,1)}), bf16[5248,512]{1,0:T(8,128)(2,1)}) %all-gather.15.cloned.1.call-update) | async-done | bytes 5373968 | tf_op jit(solution)/shard_map/all_gather | solution.py:345
  215.7 26.5 %far_pairs.9 = (f32[2,320,1536]{2,1,0:T(8,128)}, f32[2,1536,128]{2,1,0:T(8,128)}) custom-call(s32[69]{0:T(128)} %get-tuple-element.25.list_ref, bf16[16,328,512]{2,1,0:T(8,128)(2,1)} %bitcast.18, bf16[2,1536,384]{2,1,0:T(8,128)(2,1)} %get-tuple-element.27.host_ref, f32[2,320,1536]{2,1,0:T(8,128)} %get-tuple-element.40.acc_old, ...), custom_call_target="tpu_custom_call" | custom-call | flops 24159191040 | bytes 33554432 | tf_op jit(solution)/shard_map/far_pairs/pallas_call | solution.py:384
  242.2 13.9 %all-gather.13.cloned.1.call-done = bf16[5248,512]{1,0:T(8,128)(2,1)} async-done(((bf16[328,512]{1,0:T(8,128)(2,1)}), bf16[5248,512]{1,0:T(8,128)(2,1)}) %all-gather.13.cloned.1.call-update) | async-done | bytes 5373968 | tf_op jit(solution)/shard_map/all_gather | solution.py:345
  256.1 27.7 %last_pairs.1 = (f32[2,320,1536]{2,1,0:T(8,128)}, f32[8,128]{1,0:T(8,128)}) custom-call(s32[69]{0:T(128)} %get-tuple-element.25.list_ref, bf16[16,328,512]{2,1,0:T(8,128)(2,1)} %bitcast.22, bf16[2,1536,384]{2,1,0:T(8,128)(2,1)} %get-tuple-element.27.host_ref, f32[2,320,1536]{2,1,0:T(8,128)} %get-tuple-element.42.acc_old, ...), custom_call_target="tpu_custom_call" | custom-call | flops 24159191040 | bytes 33554432 | tf_op jit(solution)/shard_map/last_pairs/pallas_call | solution.py:384
  283.8 3.0 slice_bitcast_fusion
  287.0 19.5 %energy_total.1 = f32[8,128]{1,0:T(8,128)} custom-call(f32[8,128]{1,0:T(8,128)} %get-tuple-element.45.x_ref), custom_call_target="tpu_custom_call" | custom-call | tf_op jit(solution)/shard_map/energy_total/pallas_call | solution.py:396
  306.5 1.3 reduce_sum.9
  308.4 1.3 copy-done
  309.7 3.5 %join_halves.1 = f32[320,3072]{1,0:T(8,128)} custom-call(f32[2,320,1536]{2,1,0:T(8,128)} %get-tuple-element.44.mine_ref, f32[320,1536]{1,0:T(8,128)} %copy-done), custom_call_target="tpu_custom_call" | custom-call | tf_op jit(solution)/shard_map/join_halves/pallas_call | solution.py:411
  (20 shorter events, 1.8 us)
Async XLA Ops:
  7.2 7.9 %copy-start.1 = (s32[1,15]{1,0:T(1,128)S(1)}, s32[1,15]{1,0:T(1,128)}, u32[]{:S(2)}) copy-start(s32[1,15]{1,0:T(1,128)} %param.5) | copy-start | bytes 184
  7.2 60.2 %all-gather.23.cloned.1.call-start = ((), (), s32[]{:S(2)}) async-start(), calls=%async_computation.5 | async-start | bytes 5709824 | tf_op jit(solution)/shard_map/all_gather | solution.py:345
  9.1 85.3 %all-gather.21.cloned.1.call-start = ((), (), s32[]{:S(2)}) async-start(), calls=%async_computation.4 | async-start | bytes 5709824 | tf_op jit(solution)/shard_map/all_gather | solution.py:345
  12.8 122.1 %all-gather.19.cloned.1.call-start = ((), (), s32[]{:S(2)}) async-start(), calls=%async_computation.3 | async-start | bytes 5709824 | tf_op jit(solution)/shard_map/all_gather | solution.py:345
  13.6 161.7 %all-gather.17.cloned.1.call-start = ((), (), s32[]{:S(2)}) async-start(), calls=%async_computation.2 | async-start | bytes 5709824 | tf_op jit(solution)/shard_map/all_gather | solution.py:345
  14.3 201.4 %all-gather.15.cloned.1.call-start = ((), (), s32[]{:S(2)}) async-start(), calls=%async_computation.1 | async-start | bytes 5709824 | tf_op jit(solution)/shard_map/all_gather | solution.py:345
  14.9 241.2 %all-gather.13.cloned.1.call-start = ((), (), s32[]{:S(2)}) async-start(), calls=%async_computation | async-start | bytes 5709824 | tf_op jit(solution)/shard_map/all_gather | solution.py:345
  15.0 4.7 %collective-permute-start.1 = (bf16[6,328,512]{2,1,0:T(8,128)(2,1)}, bf16[6,328,512]{2,1,0:T(8,128)(2,1)S(1)}, u32[]{:S(2)}, u32[]{:S(2)}) collective-permute-start(bf16[6,328,512]{2,1,0:T(8,128)(2,1)} %get-tuple-element.24.own_ref.refs_0_), channel_id=1, source_target_pairs={{0,1},{1,0},{2,3},{3,2},{4,5},{5,4},{6,7},{7,6},{8,9},{9,8},{10,11... | collective-permute-start | bytes 6045704 | tf_op jit(solution)/shard_map/ppermute | solution.py:346
  15.1 4.0 %collective-permute-start = (s32[1,15]{1,0:T(1,128)S(1)}, s32[1,15]{1,0:T(1,128)S(1)}, u32[]{:S(2)}, u32[]{:S(2)}) collective-permute-start(s32[1,15]{1,0:T(1,128)S(1)} %copy-done.1), channel_id=1, source_target_pairs={{0,1},{1,0},{2,3},{3,2},{4,5},{5,4},{6,7},{7,6},{8,9},{9,8},{10,11... | collective-permute-start | bytes 188 | tf_op jit(solution)/shard_map/ppermute | solution.py:347
  19.7 1.3 copy-start.2
  286.7 21.7 %collective-permute-start.2 = (f32[320,1536]{1,0:T(8,128)}, f32[320,1536]{1,0:T(8,128)S(1)}, u32[]{:S(2)}, u32[]{:S(2)}) collective-permute-start(f32[320,1536]{1,0:T(8,128)} %slice_bitcast_fusion), channel_id=1, source_target_pairs={{0,1},{1,0},{2,3},{3,2},{4,5},{5,4},{6,7},{7,6},{8,9},{9,8},{10,11... | collective-permute-start | bytes 5898248 | tf_op jit(solution)/shard_map/ppermute | solution.py:395
  308.4 1.3 copy-start
Sparse Core Ops, SparseCore 0:
  9.6 44.0 all-gather.22
  55.4 38.8 all-gather.20
  96.0 38.8 all-gather.18
  136.4 38.8 all-gather.16
  176.7 38.9 all-gather.14
  217.2 38.8 all-gather.12
where the time goes:
time: 325 us; the launch traced here: 321 us
  Pallas kernels  235 us (72%)
  waiting for transfers between devices  61.6 us (19%)
  between operations  16 us (5%)
  local copies, waits for them, and re-layouts  5.56 us (2%)
    pallas_call x6, Pallas kernels, device_fn(): pl.pallas_call(functools.partial(far_kernel, last), out_shape=[acc_shape,...  160 us
    all_gather x6, waiting for transfers between devices, device_fn(): gathered = [lax.all_gather(part, 'seg') for part in parts]  56.1 us
    pallas_call x1, Pallas kernels, device_fn(): pl.pallas_call(functools.partial(near_kernel, seg_len, reach), out_shape=...  46.4 us
    pallas_call x1, Pallas kernels, device_fn(): pl.pallas_call(functools.partial(total_kernel, seg_len), out_shape=shape(...  19.5 us
  transfers between devices with their start and end apart: 9, of which 6 were waited for; matrix products, arithmetic and copies ran while one was open for 1% of the time, Pallas kernels for 63%

commit v1 on v0

--- a/solution.py
+++ b/solution.py
@@ -8,7 +8,7 @@
 from jax.experimental.pallas import tpu as pltpu
 from jax.sharding import PartitionSpec as P
 
-CHUNKS = 6
+CHUNKS = 4
 TILE = 256
 EXTRA = 8
 DEPTH = 384
@@ -88,7 +88,7 @@
 
 
 def sweep(acc_ref, sum_ref, step):
-    for number, ref, rows in ((0, acc_ref, 8), (1, sum_ref, 96)):
+    for number, ref, rows in ((0, acc_ref, 64), (1, sum_ref, 512)):
         def one(k, carry):
             step(number, (slice(None), pl.ds(pl.multiple_of(k * rows, 8), rows), slice(None)))
             return carry
@@ -182,20 +182,21 @@
         return carry
 
     def unmasked(step, carry):
-        far_step = step - CHUNKS
-        host = jnp.where(step < CHUNKS, step // per_half, far_step // CHUNKS)
-        base = jnp.where(step < CHUNKS, host * CHUNKS + (1 - core) * per_half + lax.rem(step, per_half), (1 - host) * CHUNKS + lax.rem(step, CHUNKS))
-        run(base, host, None)
+        host = jnp.where(step < 2, step, lax.rem(step, 2))
+        base = jnp.where(step < 2, host * CHUNKS + (1 - core) * per_half, (1 - host) * CHUNKS + (step // 2 - 1) * per_half)
+        for part in range(per_half):
+            run(base + part, host, None)
         return carry
 
     lax.fori_loop(0, CHUNKS, masked, 0)
     linked = band_ref[0, reach + 1 - 2 * core] != 0
-    lax.fori_loop(0, jnp.where(linked, 3 * CHUNKS, CHUNKS), unmasked, 0)
+    lax.fori_loop(0, jnp.where(linked, 6, 2), unmasked, 0)
 
 
 def far_kernel(last, list_ref, vis_ref, host_ref, acc_old, sum_old, *refs):
     if last:
-        own_ref, partner_ref, acc_ref, energy_ref, vis, charges, acc_prev, sum_prev, sems, old_sems, sum_ref, x_buf, x_sems = refs
+        (own_ref, partner_ref, out_ref, part_ref, energy_ref, vis, charges, acc_prev, sum_prev, sems, old_sems,
+         acc_ref, sum_ref, x_buf, x_sems, out_sem) = refs
     else:
         acc_ref, sum_ref, vis, charges, acc_prev, sum_prev, sems, old_sems = refs
     feat = acc_ref.shape[1]
@@ -252,7 +253,9 @@
         return
     half = acc_ref.shape[2]
     energy = jnp.zeros((8, 128), jnp.float32)
-    for host in range(2):
+    place = pl.ds(pl.multiple_of(core * half, 128), half)
+    store = pltpu.make_async_copy(acc_ref.at[0], out_ref.at[:, place], out_sem)
+    for host, target in ((0, acc_ref.at[0]), (1, part_ref)):
         sums = sum_ref[host] + sum_prev[host]
         energy = energy + jnp.sum(sums.reshape(half // 8, 8, 128), axis=0)
         total = jnp.zeros((8, half), jnp.float32)
@@ -260,23 +263,28 @@
             total = total + lax.dot_general(
                 jnp.ones((8, 128), jnp.bfloat16), piece.astype(jnp.bfloat16), (((1,), (1,)), ((), ())), preferred_element_type=jnp.float32)
         pulled = acc_ref[host] + acc_prev[host]
-        acc_ref[host] = (total[0:1] * x_buf[host].astype(jnp.float32) - pulled) * (1.0 / feat)
+        target[...] = (total[0:1] * x_buf[host].astype(jnp.float32) - pulled) * (1.0 / feat)
+        if host == 0:
+            store.start()
     energy_ref[...] = energy
+    store.wait()
 
 
 def join_kernel(mine_ref, other_ref, out_ref, bounce, sems):
     half = other_ref.shape[1]
+    pieces_n = sems.shape[1]
+    rows = other_ref.shape[0] // pieces_n
     core = lax.rem(lax.axis_index('seg'), 2)
-    sources = [mine_ref.at[0], other_ref]
-    loads = [pltpu.make_async_copy(sources[k], bounce.at[k], sems.at[0, k]) for k in range(2)]
-    for load in loads:
-        load.start()
-    stores = []
-    for k in range(2):
-        place = pl.multiple_of((core if k == 0 else 1 - core) * half, 128)
-        loads[k].wait()
-        stores.append(pltpu.make_async_copy(bounce.at[k], out_ref.at[:, pl.ds(place, half)], sems.at[1, k]))
-        stores[-1].start()
+    place = pl.ds(pl.multiple_of((1 - core) * half, 128), half)
+    loads, stores = [], []
+    for k in range(pieces_n):
+        span = pl.ds(k * rows, rows)
+        loads.append(pltpu.make_async_copy(other_ref.at[span], bounce.at[span], sems.at[0, k]))
+        stores.append(pltpu.make_async_copy(bounce.at[span], out_ref.at[span, place], sems.at[1, k]))
+        loads[-1].start()
+    for load, store in zip(loads, stores):
+        load.wait()
+        store.start()
     for store in stores:
         store.wait()
 
@@ -377,22 +385,27 @@
             ]
             if last:
                 scratch += [
+                    pltpu.VMEM(acc_shape.shape, jnp.float32),
                     pltpu.VMEM(sum_shape.shape, jnp.float32),
                     pltpu.VMEM(acc_shape.shape, jnp.bfloat16),
                     pltpu.SemaphoreType.DMA((2, CHUNKS // 2)),
+                    pltpu.SemaphoreType.DMA,
                 ]
-            acc, sums = pl.pallas_call(
+                out_shape = [shape((feat, n_rows), jnp.float32), shape((feat, half), jnp.float32), shape((8, 128), jnp.float32)]
+            else:
+                out_shape = [acc_shape, sum_shape]
+            acc, sums, *energy_part = pl.pallas_call(
                 functools.partial(far_kernel, last),
-                out_shape=[acc_shape, shape((8, 128), jnp.float32) if last else sum_shape],
+                out_shape=out_shape,
                 in_specs=[smem, any_space, vmem, any_space, any_space] + [any_space] * (2 if last else 0),
-                out_specs=[vmem, vmem],
+                out_specs=[any_space if last else vmem] + [vmem] * (len(out_shape) - 1),
                 scratch_shapes=scratch,
                 compiler_params=big,
                 cost_estimate=pl.CostEstimate(flops=20 * pair_flops, bytes_accessed=2 ** 25, transcendentals=20 * half * width),
                 name='last_pairs' if last else 'far_pairs',
             )(tasks, block, host, acc, sums, *((own, partner) if last else ()))
 
-        other = lax.ppermute(acc[1], 'seg', swap)
+        other = lax.ppermute(sums, 'seg', swap)
         energy_all = pl.pallas_call(
             functools.partial(total_kernel, seg_len),
             out_shape=shape((8, 128), jnp.float32),
@@ -405,7 +418,7 @@
             ],
             compiler_params=pltpu.CompilerParams(collective_id=0, has_side_effects=True),
             name='energy_total',
-        )(sums)
+        )(energy_part[0])
         energy = 0.5 * jnp.sum(energy_all)
 
         forces = pl.pallas_call(
@@ -413,7 +426,8 @@
             out_shape=shape((feat, n_rows), jnp.float32),
             in_specs=[any_space, any_space],
             out_specs=any_space,
-            scratch_shapes=[pltpu.VMEM((2, feat, half), jnp.float32), pltpu.SemaphoreType.DMA((2, 2))],
+            scratch_shapes=[pltpu.VMEM((feat, half), jnp.float32), pltpu.SemaphoreType.DMA((2, 4))],
+            input_output_aliases={0: 0},
             name='join_halves',
         )(acc, other)
         return forces.T, energy.reshape(1)

time: 325 us -> 328 us (level)
  the two profiles are of different devices: /device:TPU:22 before, /device:TPU:29 now
where the time goes in v1:
time: 328 us; the launch traced here: 323 us
  Pallas kernels  281 us (86%)
  waiting for transfers between devices  20.8 us (6%)
  between operations  15.7 us (5%)
    pallas_call x4, Pallas kernels, device_fn(): pl.pallas_call(functools.partial(far_kernel, last), out_shape=out_shape,...  217 us
    pallas_call x1, Pallas kernels, device_fn(): pl.pallas_call(functools.partial(near_kernel, seg_len, reach), out_shape=...  28 us
    pallas_call x1, Pallas kernels, device_fn(): pl.pallas_call(functools.partial(total_kernel, seg_len), out_shape=shape(...  27.9 us
    all_gather x4, waiting for transfers between devices, device_fn(): gathered = [lax.all_gather(part, 'seg') for part in parts]  15.9 us
  transfers between devices with their start and end apart: 7, of which 2 were waited for; matrix products, arithmetic and copies ran while one was open for 1% of the time, Pallas kernels for 68%

profile of v1, /device:TPU:29, one launch (start us, length us, event | category | flops | bytes accessed | tf_op | source)
XLA Modules:
  0.0 323.4 jit_solution(4086542933046227195)
XLA Ops:
  7.2 0.1 all-gather.15.cloned.1.call-start
  7.3 1.9 pack_first.1
  9.2 0.1 all-gather.13.cloned.1.call-start
  9.3 3.6 %pack.1 = (bf16[328,768]{1,0:T(8,128)(2,1)}, bf16[328,768]{1,0:T(8,128)(2,1)}, bf16[328,768]{1,0:T(8,128)(2,1)}, bf16[4,328,768]{2,1,0:T(8,128)(2,1)}) custom-call(bf16[320,3072]{1,0:T(8,128)(2,1)} %bitcast.9, f32[1,3072]{1,0:T(1,128)} %bitcast.12), custom_call_target="tpu_custom_call" | custom-call | tf_op jit(solution)/shard_map/pack/pallas_call | solution.py:344
  12.9 0.1 all-gather.11.cloned.1.call-start
  13.0 0.7 all-gather.11.cloned.1.call-update
  13.7 0.1 all-gather.9.cloned.1.call-start
  13.8 0.6 all-gather.9.cloned.1.call-update
  14.3 0.7 collective-permute-start.1
  15.1 0.1 collective-permute-start
  15.2 3.5 %collective-permute-done = s32[1,15]{1,0:T(1,128)S(1)} collective-permute-done((s32[1,15]{1,0:T(1,128)S(1)}, s32[1,15]{1,0:T(1,128)S(1)}, u32[]{:S(2)}, u32[]{:S(2)}) %collective-permute-start) | collective-permute-done | bytes 92 | tf_op jit(solution)/shard_map/ppermute | solution.py:355
  18.7 0.6 pad_add_fusion.band_ref
  19.3 1.3 copy-done.2
  20.7 28.0 %near_pairs.1 = (s32[69]{0:T(128)}, bf16[2,1536,384]{2,1,0:T(8,128)(2,1)}, f32[2,320,1536]{2,1,0:T(8,128)}, f32[2,1536,128]{2,1,0:T(8,128)}) custom-call(s32[2,15]{1,0:T(2,128)} %pad_add_fusion.band_ref, bf16[4,328,768]{2,1,0:T(8,128)(2,1)} %get-tuple-element.19.own_ref.refs_0_, bf16[4,328,768]{2,1,0:T(8,128)(2,1)} %copy-done.2), custom_call_target="tpu_custom_call" | custom-call | flops 28991029248 | bytes 16777216 | tf_op jit(solution)/shard_map/near_pairs/pallas_call | solution.py:362
  48.6 15.9 %all-gather.15.cloned.1.call-done = bf16[5248,768]{1,0:T(8,128)(2,1)} async-done(((bf16[328,768]{1,0:T(8,128)(2,1)}), bf16[5248,768]{1,0:T(8,128)(2,1)}) %all-gather.15.cloned.1.call-update) | async-done | bytes 8060944 | tf_op jit(solution)/shard_map/all_gather | solution.py:353
  64.5 53.5 %far_pairs.3 = (f32[2,320,1536]{2,1,0:T(8,128)}, f32[2,1536,128]{2,1,0:T(8,128)}) custom-call(s32[69]{0:T(128)} %get-tuple-element.20.list_ref, bf16[16,328,768]{2,1,0:T(8,128)(2,1)} %bitcast.13, bf16[2,1536,384]{2,1,0:T(8,128)(2,1)} %get-tuple-element.22.host_ref, f32[2,320,1536]{2,1,0:T(8,128)} %get-tuple-element.25.acc_old, ...), custom_call_target="tpu_custom_call" | custom-call | flops 36238786560 | bytes 33554432 | tf_op jit(solution)/shard_map/far_pairs/pallas_call | solution.py:397
  118.1 53.6 %far_pairs.4 = (f32[2,320,1536]{2,1,0:T(8,128)}, f32[2,1536,128]{2,1,0:T(8,128)}) custom-call(s32[69]{0:T(128)} %get-tuple-element.20.list_ref, bf16[16,328,768]{2,1,0:T(8,128)(2,1)} %bitcast.16, bf16[2,1536,384]{2,1,0:T(8,128)(2,1)} %get-tuple-element.22.host_ref, f32[2,320,1536]{2,1,0:T(8,128)} %get-tuple-element.27.acc_old, ...), custom_call_target="tpu_custom_call" | custom-call | flops 36238786560 | bytes 33554432 | tf_op jit(solution)/shard_map/far_pairs/pallas_call | solution.py:397
  171.7 53.5 %far_pairs.5 = (f32[2,320,1536]{2,1,0:T(8,128)}, f32[2,1536,128]{2,1,0:T(8,128)}) custom-call(s32[69]{0:T(128)} %get-tuple-element.20.list_ref, bf16[16,328,768]{2,1,0:T(8,128)(2,1)} %bitcast.15, bf16[2,1536,384]{2,1,0:T(8,128)(2,1)} %get-tuple-element.22.host_ref, f32[2,320,1536]{2,1,0:T(8,128)} %get-tuple-element.29.acc_old, ...), custom_call_target="tpu_custom_call" | custom-call | flops 36238786560 | bytes 33554432 | tf_op jit(solution)/shard_map/far_pairs/pallas_call | solution.py:397
  225.2 56.5 %last_pairs.1 = (f32[320,3072]{1,0:T(8,128)}, f32[320,1536]{1,0:T(8,128)}, f32[8,128]{1,0:T(8,128)}) custom-call(s32[69]{0:T(128)} %get-tuple-element.20.list_ref, bf16[16,328,768]{2,1,0:T(8,128)(2,1)} %bitcast.14, bf16[2,1536,384]{2,1,0:T(8,128)(2,1)} %get-tuple-element.22.host_ref, f32[2,320,1536]{2,1,0:T(8,128)} %get-tuple-element.31.acc_old, ...), custom_call_target="tpu_custom_call" | custom-call | flops 36238786560 | bytes 33554432 | tf_op jit(solution)/shard_map/last_pairs/pallas_call | solution.py:397
  281.8 0.4 collective-permute-start.2
  282.1 27.9 %energy_total.1 = f32[8,128]{1,0:T(8,128)} custom-call(f32[8,128]{1,0:T(8,128)} %get-tuple-element.35.x_ref), custom_call_target="tpu_custom_call" | custom-call | tf_op jit(solution)/shard_map/energy_total/pallas_call | solution.py:409
  310.1 1.3 reduce_sum.9
  312.0 1.3 copy-done
  313.3 2.4 join_halves.1
  (11 shorter events, 0.2 us)
Async XLA Ops:
  7.2 7.9 %copy-start.1 = (s32[1,15]{1,0:T(1,128)S(1)}, s32[1,15]{1,0:T(1,128)}, u32[]{:S(2)}) copy-start(s32[1,15]{1,0:T(1,128)} %param.5) | copy-start | bytes 184
  7.2 57.3 %all-gather.15.cloned.1.call-start = ((), (), s32[]{:S(2)}) async-start(), calls=%async_computation.3 | async-start | bytes 8564736 | tf_op jit(solution)/shard_map/all_gather | solution.py:353
  9.2 108.9 %all-gather.13.cloned.1.call-start = ((), (), s32[]{:S(2)}) async-start(), calls=%async_computation.2 | async-start | bytes 8564736 | tf_op jit(solution)/shard_map/all_gather | solution.py:353
  12.9 158.8 %all-gather.11.cloned.1.call-start = ((), (), s32[]{:S(2)}) async-start(), calls=%async_computation.1 | async-start | bytes 8564736 | tf_op jit(solution)/shard_map/all_gather | solution.py:353
  13.7 211.5 %all-gather.9.cloned.1.call-start = ((), (), s32[]{:S(2)}) async-start(), calls=%async_computation | async-start | bytes 8564736 | tf_op jit(solution)/shard_map/all_gather | solution.py:353
  14.3 5.0 %collective-permute-start.1 = (bf16[4,328,768]{2,1,0:T(8,128)(2,1)}, bf16[4,328,768]{2,1,0:T(8,128)(2,1)S(1)}, u32[]{:S(2)}, u32[]{:S(2)}) collective-permute-start(bf16[4,328,768]{2,1,0:T(8,128)(2,1)} %get-tuple-element.19.own_ref.refs_0_), channel_id=1, source_target_pairs={{0,1},{1,0},{2,3},{3,2},{4,5},{5,4},{6,7},{7,6},{8,9},{9,8},{10,11... | collective-permute-start | bytes 6045704 | tf_op jit(solution)/shard_map/ppermute | solution.py:354
  15.1 3.7 %collective-permute-start = (s32[1,15]{1,0:T(1,128)S(1)}, s32[1,15]{1,0:T(1,128)S(1)}, u32[]{:S(2)}, u32[]{:S(2)}) collective-permute-start(s32[1,15]{1,0:T(1,128)S(1)} %copy-done.1), channel_id=1, source_target_pairs={{0,1},{1,0},{2,3},{3,2},{4,5},{5,4},{6,7},{7,6},{8,9},{9,8},{10,11... | collective-permute-start | bytes 188 | tf_op jit(solution)/shard_map/ppermute | solution.py:355
  19.3 1.3 copy-start.2
  281.8 30.3 %collective-permute-start.2 = (f32[320,1536]{1,0:T(8,128)}, f32[320,1536]{1,0:T(8,128)S(1)}, u32[]{:S(2)}, u32[]{:S(2)}) collective-permute-start(f32[320,1536]{1,0:T(8,128)} %get-tuple-element.34), channel_id=1, source_target_pairs={{0,1},{1,0},{2,3},{3,2},{4,5},{5,4},{6,7},{7,6},{8,9},{9,8},{10,11... | collective-permute-start | bytes 5898248 | tf_op jit(solution)/shard_map/ppermute | solution.py:408
  312.0 1.3 copy-start
Sparse Core Ops, SparseCore 0:
  9.6 54.8 all-gather.14
  66.1 49.4 all-gather.12
  117.3 49.4 all-gather.10
  168.3 49.4 all-gather.8
